TPU v7x, 32 devices: a whole 2x2x4 slice. The times are simulated.
32 devices in a mesh: rows: 4 (over z), tp: 4 (over y, x), unit: 2 (over core).
Axes of the slice: x: 2, y: 2, z: 4, core: 2. Of those that a mesh axis runs over, the one named last changes fastest.
Arguments:
- w_query: bfloat16 [5120, 4096], P(('unit', 'rows'), 'tp'), parts along dimension 0, may hold values from -0.125 to 0.125
- low_query: bfloat16 [5120, 64], P(('unit', 'rows')), parts along dimension 0, may hold values from -0.125 to 0.125
- high_query: bfloat16 [128, 4096], P('unit', 'tp'), parts along dimension 0, may hold values from -0.75 to 0.75
- w_key: bfloat16 [5120, 1024], P(('unit', 'rows'), 'tp'), parts along dimension 0, may hold values from -0.125 to 0.125
- low_key: bfloat16 [5120, 64], P(('unit', 'rows')), parts along dimension 0, may hold values from -0.125 to 0.125
- high_key: bfloat16 [128, 1024], P('unit', 'tp'), parts along dimension 0, may hold values from -0.75 to 0.75
- w_value: bfloat16 [5120, 1024], P(('unit', 'rows'), 'tp'), parts along dimension 0, may hold values from -0.125 to 0.125
- low_value: bfloat16 [5120, 64], P(('unit', 'rows')), parts along dimension 0, may hold values from -0.125 to 0.125
- high_value: bfloat16 [128, 1024], P('unit', 'tp'), parts along dimension 0, may hold values from -0.75 to 0.75
- w_mixed: bfloat16 [8192, 2560], P(('unit', 'tp'), 'rows'), parts along dimension 0, may hold values from -0.09375 to 0.09375
- low_mixed: bfloat16 [8192, 64], P(('unit', 'tp')), parts along dimension 0, may hold values from -0.09375 to 0.09375
- high_mixed: bfloat16 [128, 2560], P('unit', 'rows'), parts along dimension 0, may hold values from -0.75 to 0.75
- norm_train: float32 [5120], P(('unit', 'rows', 'tp')), parts along dimension 0, may hold values from 0.25 to 1.75
- norm_step: float32 [5120], P(('unit', 'rows', 'tp')), parts along dimension 0, may hold values from -0.3 to 0.3
Outputs:
- final_query: bfloat16 [5120, 4096], P('unit', 'tp'), parts along dimension 0
- final_key: bfloat16 [5120, 1024], P('unit', 'tp'), parts along dimension 0
- final_value: bfloat16 [5120, 1024], P('unit', 'tp'), parts along dimension 0
- final_mixed: bfloat16 [8192, 2560], P(('unit', 'tp')), parts along dimension 0
- serve_norm: bfloat16 [5120], P('unit'), parts along dimension 0
There are 2 independent parts, one for each index of `unit`. A program takes and returns all parts, laid end to end along the dimension named above; each array names one. Nothing has to cross between parts.
All inputs are finite; a program needn't handle non-finite values.
Results may differ from a plain program's by a relative error of at most 0.001.
Values may be sent and summed in bfloat16 or wider, within the bound.
A program may use at most 128 MiB of HBM per device.

v0:
```python
import jax
import jax.numpy as jnp
from jax import lax
from jax.sharding import PartitionSpec as P

mix_rate = 0.5


def shards(
    w_query,
    low_query,
    high_query,
    w_key,
    low_key,
    high_key,
    w_value,
    low_value,
    high_value,
    w_mixed,
    low_mixed,
    high_mixed,
    norm_train,
    norm_step,
):
    result_query = w_query.astype(jnp.float32) + mix_rate * jnp.dot(
        low_query, high_query, preferred_element_type=jnp.float32
    )
    result_key = w_key.astype(jnp.float32) + mix_rate * jnp.dot(
        low_key, high_key, preferred_element_type=jnp.float32
    )
    result_value = w_value.astype(jnp.float32) + mix_rate * jnp.dot(
        low_value, high_value, preferred_element_type=jnp.float32
    )
    result_mixed = w_mixed.astype(jnp.float32) + mix_rate * jnp.dot(
        low_mixed, high_mixed, preferred_element_type=jnp.float32
    )
    narrow_query, narrow_key, narrow_value, narrow_mixed = (
        result_query.astype(jnp.bfloat16),
        result_key.astype(jnp.bfloat16),
        result_value.astype(jnp.bfloat16),
        result_mixed.astype(jnp.bfloat16),
    )
    final_query, final_key, final_value, final_mixed = (
        lax.all_gather(narrow_query, "rows", axis=0, tiled=True),
        lax.all_gather(narrow_key, "rows", axis=0, tiled=True),
        lax.all_gather(narrow_value, "rows", axis=0, tiled=True),
        lax.all_gather(narrow_mixed, "rows", axis=1, tiled=True),
    )
    serve_norm = lax.all_gather(
        (norm_train + norm_step).astype(jnp.bfloat16), ("rows", "tp"), axis=0, tiled=True
    )
    return (final_query, final_key, final_value, final_mixed, serve_norm)


def solution(mesh):
    return jax.shard_map(
        shards,
        mesh=mesh,
        in_specs=(
            P(("unit", "rows"), "tp"),
            P(("unit", "rows"), None),
            P("unit", "tp"),
            P(("unit", "rows"), "tp"),
            P(("unit", "rows"), None),
            P("unit", "tp"),
            P(("unit", "rows"), "tp"),
            P(("unit", "rows"), None),
            P("unit", "tp"),
            P(("unit", "tp"), "rows"),
            P(("unit", "tp"), None),
            P("unit", "rows"),
            P(("unit", "rows", "tp")),
            P(("unit", "rows", "tp")),
        ),
        out_specs=(
            P("unit", "tp"),
            P("unit", "tp"),
            P("unit", "tp"),
            P(("unit", "tp"), None),
            P("unit"),
        ),
        check_vma=False,
    )
```

profile of v0, /device:TPU:0, one launch (start us, length us, event | category | flops | bytes accessed | tf_op | source)
XLA Modules:
  0.0 295.5 jit_solution(12324406735975937253)
XLA Ops:
  7.2 0.0 copy-start
  7.2 0.0 copy-start.2
  7.2 0.0 all-gather.7.cloned.1.call-start
  7.2 2.1 fusion.2
  9.4 0.0 all-gather.7.cloned.1.call-update
  9.4 0.0 copy-start.3
  9.4 0.0 copy-start.6
  9.4 0.0 copy-start.7
  9.4 0.0 all-gather.9.cloned.1.call-start
  9.5 2.1 fusion.3
  11.6 0.0 all-gather.9.cloned.1.call-update
  11.7 0.0 all-gather.5.cloned.1.call-start
  11.7 0.0 copy-done
  11.7 0.0 copy-done.2
  11.7 2.5 add_convert_fusion.1
  14.2 0.0 copy-start.10
  14.2 0.0 copy-start.8
  14.2 0.0 copy-start.9
  14.2 0.0 all-gather.5.cloned.1.call-update
  14.2 0.0 all-gather.11.cloned.1.call-start
  14.3 0.0 copy-done.3
  14.3 0.0 copy-done.6
  14.3 0.0 copy-done.7
  14.3 1.6 add_convert_fusion
  15.9 0.0 all-gather.11.cloned.1.call-update
  15.9 0.0 copy-done.10
  15.9 0.6 dynamic-slice
  17.2 0.0 copy-done.8
  17.2 0.0 copy-done.9
  17.2 0.2 dynamic-update-slice
  17.5 46.0 %all-reduce = bf16[2560]{0:T(1024)(128)(2,1)} all-reduce(bf16[2560]{0:T(1024)(128)(2,1)S(1)} %dynamic-update-slice), channel_id=1, replica_groups=mesh['rows'=4,'tp'=4,'unit'=2] {'rows','tp'}, use_global_device_ids=true, to_apply=%add | all-reduce | flops 2560 | bytes 10240
  63.5 0.0 all-gather.7.cloned.1.call-done
  63.5 0.0 copy-start.4
  63.5 16.7 %all-gather.9.cloned.1.call-done = bf16[2560,256]{1,0:T(8,128)(2,1)} async-done(((bf16[640,256]{1,0:T(8,128)(2,1)}), bf16[2560,256]{1,0:T(8,128)(2,1)}) %all-gather.9.cloned.1.call-update) | async-done | bytes 1310736 | tf_op jit(solution)/shard_map/all_gather | solution.py:46
  80.3 99.4 %all-gather.5.cloned.1.call-done = bf16[2560,1024]{1,0:T(8,128)(2,1)} async-done(((bf16[640,1024]{1,0:T(8,128)(2,1)}), bf16[2560,1024]{1,0:T(8,128)(2,1)}) %all-gather.5.cloned.1.call-update) | async-done | bytes 5242896 | tf_op jit(solution)/shard_map/all_gather | solution.py:44
  179.7 98.4 %all-gather.11.cloned.1.call-done = bf16[1024,2560]{1,0:T(8,128)(2,1)} async-done(((bf16[1024,640]{1,0:T(8,128)(2,1)}), bf16[1024,2560]{1,0:T(8,128)(2,1)}) %all-gather.11.cloned.1.call-update) | async-done | bytes 5242896 | tf_op jit(solution)/shard_map/all_gather | solution.py:47
  278.1 0.0 copy-start.1
  278.1 5.6 %copy.24 = bf16[2560,1024]{1,0:T(8,128)(2,1)} copy(bf16[2560,1024]{1,0:T(8,128)(2,1)} %all-gather.5.cloned.1.call-done) | data formatting | bytes 10485760
  283.7 0.0 copy-done.4
  283.7 0.0 copy-start.5
  283.7 1.1 copy.25
  284.8 0.7 copy-done.5
  285.5 1.1 copy.26
  286.6 0.0 copy-done.1
  286.6 2.4 copy.27
  (2 shorter events, 0.0 us)
Async XLA Ops:
  7.2 4.5 %copy-start = (bf16[64,1024]{1,0:T(8,128)(2,1)S(1)}, bf16[64,1024]{1,0:T(8,128)(2,1)}, u32[]{:S(2)}) copy-start(bf16[64,1024]{1,0:T(8,128)(2,1)} %param.16) | copy-start | bytes 393220
  7.2 4.5 %copy-start.2 = (bf16[640,1024]{1,0:T(8,128)(2,1)S(1)}, bf16[640,1024]{1,0:T(8,128)(2,1)}, u32[]{:S(2)}) copy-start(bf16[640,1024]{1,0:T(8,128)(2,1)} %param.14) | copy-start | bytes 3932164
  7.2 56.3 %all-gather.7.cloned.1.call-start = ((), (), s32[]{:S(2)}) async-start(), calls=%async_computation.1 | async-start | bytes 1638400 | tf_op jit(solution)/shard_map/all_gather | solution.py:45
  9.4 4.9 %copy-start.3 = (bf16[1024,640]{1,0:T(8,128)(2,1)S(1)}, bf16[1024,640]{1,0:T(8,128)(2,1)}, u32[]{:S(2)}) copy-start(bf16[1024,640]{1,0:T(8,128)(2,1)} %param.23) | copy-start | bytes 3932164
  9.4 4.9 %copy-start.6 = (bf16[1024,64]{0,1:T(8,128)(2,1)S(1)}, bf16[1024,64]{0,1:T(8,128)(2,1)}, u32[]{:S(2)}) copy-start(bf16[1024,64]{0,1:T(8,128)(2,1)} %param.24) | copy-start | bytes 393220
  9.4 4.9 %copy-start.7 = (bf16[64,640]{1,0:T(8,128)(2,1)S(1)}, bf16[64,640]{1,0:T(8,128)(2,1)}, u32[]{:S(2)}) copy-start(bf16[64,640]{1,0:T(8,128)(2,1)} %param.25) | copy-start | bytes 245764
  9.4 70.8 %all-gather.9.cloned.1.call-start = ((), (), s32[]{:S(2)}) async-start(), calls=%async_computation.2 | async-start | bytes 1638400 | tf_op jit(solution)/shard_map/all_gather | solution.py:46
  11.7 168.0 %all-gather.5.cloned.1.call-start = ((), (), s32[]{:S(2)}) async-start(), calls=%async_computation | async-start | bytes 6553600 | tf_op jit(solution)/shard_map/all_gather | solution.py:44
  14.2 1.7 copy-start.10
  14.2 3.0 %copy-start.8 = (f32[160]{0:T(256)S(1)}, f32[160]{0:T(256)}, u32[]{:S(2)}) copy-start(f32[160]{0:T(256)} %param.26) | copy-start | bytes 1924
  14.2 3.0 %copy-start.9 = (f32[160]{0:T(256)S(1)}, f32[160]{0:T(256)}, u32[]{:S(2)}) copy-start(f32[160]{0:T(256)} %param.27) | copy-start | bytes 1924
  14.2 263.9 %all-gather.11.cloned.1.call-start = ((), (), s32[]{:S(2)}) async-start(), calls=%async_computation.3 | async-start | bytes 6553600 | tf_op jit(solution)/shard_map/all_gather | solution.py:47
  63.5 220.2 %copy-start.4 = (bf16[2560,256]{1,0:T(8,128)(2,1)S(1)}, bf16[2560,256]{1,0:T(8,128)(2,1)}, u32[]{:S(2)}) copy-start(bf16[2560,256]{1,0:T(8,128)(2,1)} %all-gather.7.cloned.1.call-done) | copy-start | bytes 3932164
  278.1 8.5 %copy-start.1 = (bf16[1024,2560]{1,0:T(8,128)(2,1)S(1)}, bf16[1024,2560]{1,0:T(8,128)(2,1)}, u32[]{:S(2)}) copy-start(bf16[1024,2560]{1,0:T(8,128)(2,1)} %all-gather.11.cloned.1.call-done) | copy-start | bytes 15728644
  283.7 1.8 copy-start.5
Sparse Core Ops, SparseCore 0:
  10.1 36.3 all-gather.6
  48.7 31.4 all-gather.8
  82.4 97.2 all-gather.4
  181.7 96.3 all-gather.10
where the time goes:
time: 296 us; the launch traced here: 295 us
  waiting for transfers between devices  215 us (73%)
  blocking collectives  46 us (16%)
  between operations  14.5 us (5%)
  local copies, waits for them, and re-layouts  11.7 us (4%)
  matrix products  8.35 us (3%)
    all_gather x1, waiting for transfers between devices, shards(): lax.all_gather(narrow_query, 'rows', axis=0, tiled=True)  99.4 us
    all_gather x1, waiting for transfers between devices, shards(): lax.all_gather(narrow_mixed, 'rows', axis=1, tiled=True)  98.4 us
    unnamed x1, blocking collectives  46 us
    all_gather x1, waiting for transfers between devices, shards(): lax.all_gather(narrow_value, 'rows', axis=0, tiled=True)  16.7 us
    unnamed x29, local copies, waits for them, and re-layouts  11.7 us
  transfers between devices with their start and end apart: 4, of which 3 were waited for; matrix products, arithmetic and copies ran while one was open for 2% of the time, Pallas kernels for 0%

commit v1 on v0

v1 whole, which is shorter than its diff:
```python
import functools

import jax
import jax.numpy as jnp
from jax import lax
from jax.experimental import pallas as pl
from jax.experimental.pallas import tpu as pltpu
from jax.sharding import PartitionSpec as P

MESH = pl.DeviceIdType.MESH
mix_rate = 0.5
chunk_bytes = 400 * 1024


def pieces_of(rows, columns):
    count = 1
    while rows * columns * 2 > count * chunk_bytes and rows % (count * 32) == 0:
        count *= 2
    return count


def block_of(size, options):
    for option in options:
        if size % option == 0:
            return option
    return size


def kernel(n, tps, stacked, pieces, *refs):
    kinds = len(pieces)
    w, low, high = refs[:kinds], refs[kinds : 2 * kinds], refs[2 * kinds : 3 * kinds]
    norm_train, norm_step = refs[3 * kinds : 3 * kinds + 2]
    refs = refs[3 * kinds + 2 :]
    out, norm_out = refs[:kinds], refs[kinds]
    refs = refs[kinds + 1 :]
    w_own, low_own, high_own = refs[:kinds], refs[kinds : 2 * kinds], refs[2 * kinds : 3 * kinds]
    refs = refs[3 * kinds :]
    norm_all, load_sem, side_sem, send_sem, recv_sem, norm_send, norm_recv, cross_send, cross_recv = refs

    z, t = lax.axis_index("rows"), lax.axis_index("tp")
    chunks = [(k, p) for k in range(kinds) for p in range(pieces[k])]
    has_up, has_down = z < n - 1, z > 0

    barrier = pltpu.get_barrier_semaphore()

    @pl.when(has_up)
    def _():
        pl.semaphore_signal(barrier, inc=1, device_id={"rows": z + 1}, device_id_type=MESH)

    @pl.when(has_down)
    def _():
        pl.semaphore_signal(barrier, inc=1, device_id={"rows": z - 1}, device_id_type=MESH)

    for step in range(1, tps):
        pl.semaphore_signal(barrier, inc=1, device_id={"tp": lax.rem(t + step, tps)}, device_id_type=MESH)

    def rows_of(k, p):
        size = w[k].shape[0] // pieces[k]
        return p * size, size

    def load(i):
        k, p = chunks[i]
        start, size = rows_of(k, p)
        return pltpu.make_async_copy(
            w[k].at[pl.ds(start, size)], w_own[k].at[pl.ds(start, size)], load_sem.at[i]
        )

    def side(k):
        return (
            pltpu.make_async_copy(low[k], low_own[k], side_sem.at[0, k]),
            pltpu.make_async_copy(high[k], high_own[k], side_sem.at[1, k]),
        )

    for i, (k, p) in enumerate(chunks):
        if p == 0:
            for copy in side(k):
                copy.start()
        load(i).start()

    def region(k, p, origin):
        start, size = rows_of(k, p)
        columns = w[k].shape[1]
        if stacked[k]:
            return out[k].at[origin, pl.ds(start, size)]
        if out[k].shape[1] == columns:
            rows = w[k].shape[0]
            return out[k].at[pl.ds(pl.multiple_of(origin * rows + start, 16), size)]
        return out[k].at[pl.ds(start, size), pl.ds(pl.multiple_of(origin * columns, 128), columns)]

    def hop(i, origin, direction):
        k, p = chunks[i]
        place = region(k, p, origin)
        return pltpu.make_async_remote_copy(
            src_ref=place,
            dst_ref=place,
            send_sem=send_sem.at[direction, origin, i],
            recv_sem=recv_sem.at[direction, origin, i],
            device_id={"rows": z + 1 - 2 * direction},
            device_id_type=MESH,
        )

    def norm_hop(origin, direction):
        return pltpu.make_async_remote_copy(
            src_ref=norm_all.at[origin, t],
            dst_ref=norm_all.at[origin, t],
            send_sem=norm_send.at[direction, origin],
            recv_sem=norm_recv.at[direction, origin],
            device_id={"rows": z + 1 - 2 * direction},
            device_id_type=MESH,
        )

    def cross(step, column):
        return pltpu.make_async_remote_copy(
            src_ref=norm_all.at[:, column],
            dst_ref=norm_all.at[:, column],
            send_sem=cross_send.at[step],
            recv_sem=cross_recv.at[step],
            device_id={"tp": lax.rem(t + step, tps)},
            device_id_type=MESH,
        )

    def send_both(make):
        @pl.when(has_up)
        def _():
            make(0).start()

        @pl.when(has_down)
        def _():
            make(1).start()

    def merge(i):
        k, p = chunks[i]
        start, size = rows_of(k, p)
        columns = w[k].shape[1]
        high_block = block_of(size, (160, 128, 64, 32, 16))
        wide_block = block_of(columns, (256, 128))
        wides = columns // wide_block
        place = region(k, p, z)

        def body(b, _):
            if size == high_block:
                r, c = 0, b
            else:
                r, c = b // wides, b % wides
            r = r * high_block
            c = 0 if wides == 1 else pl.multiple_of(c * wide_block, wide_block)
            mine = pl.ds(start + r, high_block)
            wide = pl.ds(c, wide_block)
            result = w_own[k][mine, wide].astype(jnp.float32) + mix_rate * jnp.dot(
                low_own[k][mine, :], high_own[k][:, wide], preferred_element_type=jnp.float32
            )
            place[pl.ds(r, high_block), wide] = result.astype(jnp.bfloat16)
            return 0

        lax.fori_loop(0, (size // high_block) * wides, body, 0)

    norm = (norm_train[...] + norm_step[...]).astype(jnp.bfloat16).astype(jnp.float32)
    norm_all[z, t] = norm

    for i, (k, p) in enumerate(chunks):
        if p == 0:
            for copy in side(k):
                copy.wait()
        load(i).wait()
        merge(i)
        if i == 0:
            partners = has_up.astype(jnp.int32) + has_down.astype(jnp.int32) + tps - 1
            pl.semaphore_wait(barrier, partners)
        else:
            send_both(functools.partial(hop, i - 1, z))
    send_both(functools.partial(hop, len(chunks) - 1, z))
    send_both(functools.partial(norm_hop, z))

    def arrival(make, d):
        below, above = z - d, z + d

        @pl.when(below >= 0)
        def _():
            make(below, 0).wait_recv()

            @pl.when(has_up)
            def _():
                make(below, 0).start()

        @pl.when(above < n)
        def _():
            make(above, 1).wait_recv()

            @pl.when(has_down)
            def _():
                make(above, 1).start()

    def distance(d, _):
        for i in range(len(chunks)):
            arrival(functools.partial(hop, i), d)
        arrival(norm_hop, d)
        return 0

    def all_norms():
        for step in range(1, tps):
            cross(step, t).start()
        for step in range(1, tps):
            cross(step, lax.rem(t + tps - step, tps)).wait_recv()
        norm_out[...] = jnp.concatenate(
            [norm_all[a, b] for a in range(n) for b in range(tps)], axis=1
        ).astype(jnp.bfloat16)

    lax.fori_loop(1, n, distance, 0)
    all_norms()

    def drain(origin, _):
        for direction, flag in ((0, has_up & (origin <= z)), (1, has_down & (origin >= z))):

            @pl.when(flag)
            def _():
                for i in range(len(chunks)):
                    hop(i, origin, direction).wait_send()
                norm_hop(origin, direction).wait_send()

        return 0

    lax.fori_loop(0, n, drain, 0)
    for step in range(1, tps):
        cross(step, t).wait_send()


def shards(n, tps, *args):
    w, low, high = args[0:12:3], args[1:12:3], args[2:12:3]
    norm_train, norm_step = args[12].reshape(1, -1), args[13].reshape(1, -1)
    kinds = len(w)
    by_column = [False] * (kinds - 1) + [True]
    stacked = [by_column[k] and w[k].shape[1] % 128 != 0 for k in range(kinds)]
    pieces = [pieces_of(*w[k].shape) for k in range(kinds)]
    count = sum(pieces)
    shapes = []
    for k in range(kinds):
        rows, columns = w[k].shape
        if stacked[k]:
            shapes.append((n, rows, columns))
        elif by_column[k]:
            shapes.append((rows, n * columns))
        else:
            shapes.append((n * rows, columns))
    share = norm_train.shape[1]
    vmem, anywhere = pl.BlockSpec(memory_space=pltpu.VMEM), pl.BlockSpec(memory_space=pl.ANY)
    dma = pltpu.SemaphoreType.DMA
    results = pl.pallas_call(
        functools.partial(kernel, n, tps, stacked, pieces),
        out_shape=[jax.ShapeDtypeStruct(s, jnp.bfloat16) for s in shapes]
        + [jax.ShapeDtypeStruct((1, n * tps * share), jnp.bfloat16)],
        in_specs=[anywhere] * (3 * kinds) + [vmem] * 2,
        out_specs=[vmem] * (kinds + 1),
        scratch_shapes=[pltpu.VMEM(x.shape, x.dtype) for x in (*w, *low, *high)]
        + [
            pltpu.VMEM((n, tps, 1, share), jnp.float32),
            dma((count,)),
            dma((2, kinds)),
            dma((2, n, count)),
            dma((2, n, count)),
            dma((2, n)),
            dma((2, n)),
            dma((tps,)),
            dma((tps,)),
        ],
        compiler_params=pltpu.CompilerParams(
            collective_id=0, has_side_effects=True, vmem_limit_bytes=28 * 1024 * 1024
        ),
        name="merge_and_gather",
    )(*w, *low, *high, norm_train, norm_step)
    finals = []
    for k in range(kinds):
        full = results[k]
        if stacked[k]:
            full = full.transpose(1, 0, 2).reshape(full.shape[1], -1)
        finals.append(full)
    return (*finals, results[kinds].reshape(-1))


def solution(mesh):
    return jax.shard_map(
        functools.partial(shards, mesh.shape["rows"], mesh.shape["tp"]),
        mesh=mesh,
        in_specs=(
            P(("unit", "rows"), "tp"),
            P(("unit", "rows"), None),
            P("unit", "tp"),
            P(("unit", "rows"), "tp"),
            P(("unit", "rows"), None),
            P("unit", "tp"),
            P(("unit", "rows"), "tp"),
            P(("unit", "rows"), None),
            P("unit", "tp"),
            P(("unit", "tp"), "rows"),
            P(("unit", "tp"), None),
            P("unit", "rows"),
            P(("unit", "rows", "tp")),
            P(("unit", "rows", "tp")),
        ),
        out_specs=(
            P("unit", "tp"),
            P("unit", "tp"),
            P("unit", "tp"),
            P(("unit", "tp"), None),
            P("unit"),
        ),
        check_vma=False,
    )
```

time: 296 us -> 254 us (0.86)
  Pallas kernels: 0 us -> 224 us
  waiting for transfers between devices: 215 us -> 0 us
  blocking collectives: 46 us -> 0 us
  local copies, waits for them, and re-layouts: 11.7 us -> 28.2 us
  between operations: 14.5 us -> 0.68 us
  matrix products: 8.35 us -> 0 us
    pallas_call x0 -> x1, Pallas kernels: none -> 224 us  [shards(): pl.pallas_call(functools.partial(kernel, n, tps, stacked, pieces), out_sh...]
    all_gather x4 -> x0, waiting for transfers between devices: 215 us -> none  [the longest x1 99.4 us: shards(): lax.all_gather(narrow_query, 'rows', axis=0, tiled=True)]
    unnamed x1 -> x0, blocking collectives: 46 us -> none
    unnamed x29 -> x34, local copies, waits for them, and re-layouts: 11.7 us -> 28.2 us
    dot_general x4 -> x0, matrix products: 8.35 us -> none  [the longest x1 2.47 us: shards(): jnp.dot(low_query, high_query, preferred_element_type=jnp.float32)]
  transfers between devices with their start and end apart: 4 -> 0, of which waited for: 3 -> 0; matrix products, arithmetic and copies ran while one was open for 2% -> 0% of each run, Pallas kernels for 0% -> 0%
where the time goes in v1:
time: 254 us; the launch traced here: 253 us
  Pallas kernels  224 us (88%)
  local copies, waits for them, and re-layouts  28.2 us (11%)
    pallas_call x1, Pallas kernels, shards(): pl.pallas_call(functools.partial(kernel, n, tps, stacked, pieces), out_sh...  224 us
    unnamed x34, local copies, waits for them, and re-layouts  28.2 us

profile of v1, /device:TPU:0, one launch (start us, length us, event | category | flops | bytes accessed | tf_op | source)
XLA Modules:
  0.0 253.4 jit_solution(1510614475921670639)
XLA Ops:
  0.6 1.0 copy.19.refs_4_
  1.7 1.1 copy.20.refs_5_
  2.7 1.1 copy.21.refs_6_
  3.8 1.1 copy.22.refs_7_
  4.9 0.0 copy-start.3
  4.9 1.3 copy-done.3
  6.2 0.0 copy-start.4
  6.2 1.3 copy-done.4
  7.5 0.0 copy-start.5
  7.5 1.0 copy-done.5
  8.5 0.0 copy-start.6
  8.5 1.0 copy-done.6
  9.5 0.0 copy-start.7
  9.5 0.9 copy-done.7
  10.4 0.0 copy-start.8
  10.4 0.9 copy-done.8
  11.3 0.0 copy-start.9
  11.3 0.8 copy-done.9
  12.0 0.0 copy-start.10
  12.0 0.8 copy-done.10
  12.8 0.0 copy-start.11
  12.8 0.7 copy-done.11
  13.5 0.0 copy-start.12
  13.5 0.7 copy-done.12
  14.1 223.9 %merge_and_gather.1 = (bf16[2560,1024]{1,0:T(8,128)(2,1)S(1)}, bf16[2560,256]{1,0:T(8,128)(2,1)S(1)}, bf16[2560,256]{1,0:T(8,128)(2,1)S(1)}, bf16[1024,2560]{1,0:T(8,128)(2,1)S(1)}, bf16[1,2560]{1,0:T(2,128)(2,1)S(1)}) custom-call(bf16[640,1024]{1,0:T(8,128)(2,1)S(1)} %copy-done.3, bf16[640,256]{1,0:T(8,128)(2,1)S(1)} %copy-done.5, ...), custom_call_target="tpu_custom_call" | custom-call | tf_op jit(solution)/shard_map/merge_and_gather/pallas_call | solution.py:247
  238.1 0.0 copy-start
  238.1 2.3 copy-done
  240.4 0.0 copy-start.2
  240.4 2.4 copy-done.2
  242.7 0.6 reduce
  243.4 0.0 copy-start.1
  243.4 5.6 %copy.27 = bf16[2560,1024]{1,0:T(8,128)(2,1)} copy(bf16[2560,1024]{1,0:T(8,128)(2,1)} %copy-done.2) | data formatting | bytes 10485760
  249.0 1.1 copy.28
  250.0 1.1 copy.29
  251.1 0.0 copy-done.1
  251.1 2.4 copy.30
Async XLA Ops:
  4.9 1.3 copy-start.3
  6.2 1.3 copy-start.4
  7.5 1.0 copy-start.5
  8.5 1.0 copy-start.6
  9.5 0.9 copy-start.7
  10.4 0.9 copy-start.8
  11.3 0.8 copy-start.9
  12.0 0.8 copy-start.10
  12.8 0.7 copy-start.11
  13.5 0.7 copy-start.12
  238.1 2.3 copy-start
  240.4 2.4 copy-start.2
  243.4 7.7 %copy-start.1 = (bf16[1024,2560]{1,0:T(8,128)(2,1)S(1)}, bf16[1024,2560]{1,0:T(8,128)(2,1)}, u32[]{:S(2)}) copy-start(bf16[1024,2560]{1,0:T(8,128)(2,1)} %copy-done) | copy-start | bytes 15728644

commit v2 on v1

--- a/solution.py
+++ b/solution.py
@@ -10,11 +10,13 @@
 MESH = pl.DeviceIdType.MESH
 mix_rate = 0.5
 chunk_bytes = 400 * 1024
-
-
-def pieces_of(rows, columns):
+first_bytes = 100 * 1024
+order = (1, 0, 3, 2)
+
+
+def pieces_of(rows, columns, most):
     count = 1
-    while rows * columns * 2 > count * chunk_bytes and rows % (count * 32) == 0:
+    while rows * columns * 2 > count * most and rows % (count * 32) == 0:
         count *= 2
     return count
 
@@ -34,11 +36,12 @@
     out, norm_out = refs[:kinds], refs[kinds]
     refs = refs[kinds + 1 :]
     w_own, low_own, high_own = refs[:kinds], refs[kinds : 2 * kinds], refs[2 * kinds : 3 * kinds]
-    refs = refs[3 * kinds :]
-    norm_all, load_sem, side_sem, send_sem, recv_sem, norm_send, norm_recv, cross_send, cross_recv = refs
+    low_rows = refs[3 * kinds : 4 * kinds]
+    refs = refs[4 * kinds :]
+    norm_own, norm_all, norm_sem, load_sem, side_sem, send_sem, recv_sem, norm_send, norm_recv, cross_send, cross_recv = refs
 
     z, t = lax.axis_index("rows"), lax.axis_index("tp")
-    chunks = [(k, p) for k in range(kinds) for p in range(pieces[k])]
+    chunks = [(k, p) for k in order for p in range(pieces[k])]
     has_up, has_down = z < n - 1, z > 0
 
     barrier = pltpu.get_barrier_semaphore()
@@ -76,6 +79,13 @@
             for copy in side(k):
                 copy.start()
         load(i).start()
+
+    norm_loads = [
+        pltpu.make_async_copy(source, norm_own.at[j], norm_sem.at[j])
+        for j, source in enumerate((norm_train, norm_step))
+    ]
+    for copy in norm_loads:
+        copy.start()
 
     def region(k, p, origin):
         start, size = rows_of(k, p)
@@ -147,20 +157,18 @@
             mine = pl.ds(start + r, high_block)
             wide = pl.ds(c, wide_block)
             result = w_own[k][mine, wide].astype(jnp.float32) + mix_rate * jnp.dot(
-                low_own[k][mine, :], high_own[k][:, wide], preferred_element_type=jnp.float32
+                low_rows[k][mine, :], high_own[k][:, wide], preferred_element_type=jnp.float32
             )
             place[pl.ds(r, high_block), wide] = result.astype(jnp.bfloat16)
             return 0
 
         lax.fori_loop(0, (size // high_block) * wides, body, 0)
-
-    norm = (norm_train[...] + norm_step[...]).astype(jnp.bfloat16).astype(jnp.float32)
-    norm_all[z, t] = norm
 
     for i, (k, p) in enumerate(chunks):
         if p == 0:
             for copy in side(k):
                 copy.wait()
+            low_rows[k][...] = low_own[k][...].astype(jnp.float32).T.astype(jnp.bfloat16)
         load(i).wait()
         merge(i)
         if i == 0:
@@ -168,8 +176,13 @@
             pl.semaphore_wait(barrier, partners)
         else:
             send_both(functools.partial(hop, i - 1, z))
+        if i == 1:
+            for copy in norm_loads:
+                copy.wait()
+            norm_all[z, t] = (norm_own[0] + norm_own[1]).astype(jnp.bfloat16).astype(jnp.float32)
+        if i == min(2, len(chunks) - 1):
+            send_both(functools.partial(norm_hop, z))
     send_both(functools.partial(hop, len(chunks) - 1, z))
-    send_both(functools.partial(norm_hop, z))
 
     def arrival(make, d):
         below, above = z - d, z + d
@@ -191,14 +204,24 @@
                 make(above, 1).start()
 
     def distance(d, _):
+        arrival(norm_hop, d)
+
+        @pl.when(d == n - 1)
+        def _():
+            for step in range(1, tps):
+                cross(step, t).start()
+
         for i in range(len(chunks)):
+            if i == len(chunks) // 2:
+
+                @pl.when(d == n - 1)
+                def _():
+                    all_norms()
+
             arrival(functools.partial(hop, i), d)
-        arrival(norm_hop, d)
         return 0
 
     def all_norms():
-        for step in range(1, tps):
-            cross(step, t).start()
         for step in range(1, tps):
             cross(step, lax.rem(t + tps - step, tps)).wait_recv()
         norm_out[...] = jnp.concatenate(
@@ -206,7 +229,6 @@
         ).astype(jnp.bfloat16)
 
     lax.fori_loop(1, n, distance, 0)
-    all_norms()
 
     def drain(origin, _):
         for direction, flag in ((0, has_up & (origin <= z)), (1, has_down & (origin >= z))):
@@ -224,13 +246,41 @@
         cross(step, t).wait_send()
 
 
+def put(parts, *refs):
+    kinds = len(parts)
+    src, dst, sem = refs[:kinds], refs[kinds : 2 * kinds], refs[2 * kinds]
+    copies = []
+    for k in range(kinds):
+        size = src[k].shape[0] // parts[k]
+        for p in range(parts[k]):
+            rows = pl.ds(p * size, size)
+            copies.append(pltpu.make_async_copy(src[k].at[rows], dst[k].at[rows], sem.at[len(copies)]))
+    for copy in copies:
+        copy.start()
+    for copy in copies:
+        copy.wait()
+
+
+def place(arrays):
+    parts = [4 if x.shape[0] % 128 == 0 else 1 for x in arrays]
+    return pl.pallas_call(
+        functools.partial(put, parts),
+        out_shape=[jax.ShapeDtypeStruct(x.shape, x.dtype) for x in arrays],
+        in_specs=[pl.BlockSpec(memory_space=pltpu.VMEM)] * len(arrays),
+        out_specs=[pl.BlockSpec(memory_space=pltpu.HBM)] * len(arrays),
+        scratch_shapes=[pltpu.SemaphoreType.DMA((sum(parts),))],
+        compiler_params=pltpu.CompilerParams(vmem_limit_bytes=24 * 1024 * 1024),
+        name="place",
+    )(*arrays)
+
+
 def shards(n, tps, *args):
-    w, low, high = args[0:12:3], args[1:12:3], args[2:12:3]
+    w, low, high = args[0:12:3], [x.T for x in args[1:12:3]], args[2:12:3]
     norm_train, norm_step = args[12].reshape(1, -1), args[13].reshape(1, -1)
     kinds = len(w)
     by_column = [False] * (kinds - 1) + [True]
     stacked = [by_column[k] and w[k].shape[1] % 128 != 0 for k in range(kinds)]
-    pieces = [pieces_of(*w[k].shape) for k in range(kinds)]
+    pieces = [pieces_of(*w[k].shape, first_bytes if k == order[0] else chunk_bytes) for k in range(kinds)]
     count = sum(pieces)
     shapes = []
     for k in range(kinds):
@@ -242,17 +292,21 @@
         else:
             shapes.append((n * rows, columns))
     share = norm_train.shape[1]
-    vmem, anywhere = pl.BlockSpec(memory_space=pltpu.VMEM), pl.BlockSpec(memory_space=pl.ANY)
+    vmem, hbm = pl.BlockSpec(memory_space=pltpu.VMEM), pl.BlockSpec(memory_space=pltpu.HBM)
     dma = pltpu.SemaphoreType.DMA
+    operands = (*w, *low, *high, norm_train, norm_step)
     results = pl.pallas_call(
         functools.partial(kernel, n, tps, stacked, pieces),
-        out_shape=[jax.ShapeDtypeStruct(s, jnp.bfloat16) for s in shapes]
-        + [jax.ShapeDtypeStruct((1, n * tps * share), jnp.bfloat16)],
-        in_specs=[anywhere] * (3 * kinds) + [vmem] * 2,
+        out_shape=[pltpu.VMEM(s, jnp.bfloat16) for s in shapes]
+        + [pltpu.VMEM((1, n * tps * share), jnp.bfloat16)],
+        in_specs=[hbm] * (3 * kinds + 2),
         out_specs=[vmem] * (kinds + 1),
         scratch_shapes=[pltpu.VMEM(x.shape, x.dtype) for x in (*w, *low, *high)]
+        + [pltpu.VMEM(x.shape[::-1], x.dtype) for x in low]
         + [
+            pltpu.VMEM((2, 1, share), jnp.float32),
             pltpu.VMEM((n, tps, 1, share), jnp.float32),
+            dma((2,)),
             dma((count,)),
             dma((2, kinds)),
             dma((2, n, count)),
@@ -263,10 +317,11 @@
             dma((tps,)),
         ],
         compiler_params=pltpu.CompilerParams(
-            collective_id=0, has_side_effects=True, vmem_limit_bytes=28 * 1024 * 1024
+            collective_id=0, has_side_effects=True, vmem_limit_bytes=24 * 1024 * 1024
         ),
         name="merge_and_gather",
-    )(*w, *low, *high, norm_train, norm_step)
+    )(*[pltpu.with_memory_space_constraint(x, pltpu.HBM) for x in operands])
+    results = place(results)
     finals = []
     for k in range(kinds):
         full = results[k]

time: 254 us -> 226 us (0.89)
  local copies, waits for them, and re-layouts: 28.2 us -> 0 us
    unnamed x34 -> x0, local copies, waits for them, and re-layouts: 28.2 us -> none
    pallas_call x0 -> x1, Pallas kernels: none -> 4.91 us  [place(): pl.pallas_call(functools.partial(put, parts), out_shape=[jax.ShapeDtypeSt...]
    pallas_call x1, Pallas kernels: 224 us -> 219 us  [shards(): pl.pallas_call(functools.partial(kernel, n, tps, stacked, pieces), out_sh...]
where the time goes in v2:
time: 226 us; the launch traced here: 225 us
  Pallas kernels  224 us (99%)
    pallas_call x1, Pallas kernels, shards(): pl.pallas_call(functools.partial(kernel, n, tps, stacked, pieces), out_sh...  219 us
    pallas_call x1, Pallas kernels, place(): pl.pallas_call(functools.partial(put, parts), out_shape=[jax.ShapeDtypeSt...  4.91 us

profile of v2, /device:TPU:0, one launch (start us, length us, event | category | flops | bytes accessed | tf_op | source)
XLA Modules:
  0.0 225.5 jit_solution(6966774036409040928)
XLA Ops:
  0.6 219.3 %merge_and_gather.1 = (bf16[2560,1024]{1,0:T(8,128)(2,1)S(1)}, bf16[2560,256]{1,0:T(8,128)(2,1)S(1)}, bf16[2560,256]{1,0:T(8,128)(2,1)S(1)}, bf16[1024,2560]{1,0:T(8,128)(2,1)S(1)}, bf16[1,2560]{1,0:T(2,128)(2,1)S(1)}) custom-call(bf16[640,1024]{1,0:T(8,128)(2,1)} %refs_0_.1, bf16[640,256]{1,0:T(8,128)(2,1)} %refs_1_.1, bf16[640,256]{1,0:T(8,128)(2,1)} %refs_2_.1, ...), custom_call_target="tpu_custom_call" | custom-call | tf_op jit(solution)/shard_map/merge_and_gather/pallas_call | solution.py:298
  219.9 4.9 %place.1 = (bf16[2560,1024]{1,0:T(8,128)(2,1)}, bf16[2560,256]{1,0:T(8,128)(2,1)}, bf16[2560,256]{1,0:T(8,128)(2,1)}, bf16[1024,2560]{1,0:T(8,128)(2,1)}, bf16[1,2560]{1,0:T(2,128)(2,1)S(1)}) custom-call(bf16[2560,1024]{1,0:T(8,128)(2,1)S(1)} %get-tuple-element.15.refs_0_, bf16[2560,256]{1,0:T(8,128)(2,1)S(1)} %get-tuple-element.16.refs_1_, ...), custom_call_target="tpu_custom_call" | custom-call | tf_op jit(solution)/shard_map/place/pallas_call | solution.py:266
  224.8 0.6 reduce

commit v3 on v2

--- a/solution.py
+++ b/solution.py
@@ -44,19 +44,6 @@
     chunks = [(k, p) for k in order for p in range(pieces[k])]
     has_up, has_down = z < n - 1, z > 0
 
-    barrier = pltpu.get_barrier_semaphore()
-
-    @pl.when(has_up)
-    def _():
-        pl.semaphore_signal(barrier, inc=1, device_id={"rows": z + 1}, device_id_type=MESH)
-
-    @pl.when(has_down)
-    def _():
-        pl.semaphore_signal(barrier, inc=1, device_id={"rows": z - 1}, device_id_type=MESH)
-
-    for step in range(1, tps):
-        pl.semaphore_signal(barrier, inc=1, device_id={"tp": lax.rem(t + step, tps)}, device_id_type=MESH)
-
     def rows_of(k, p):
         size = w[k].shape[0] // pieces[k]
         return p * size, size
@@ -74,11 +61,30 @@
             pltpu.make_async_copy(high[k], high_own[k], side_sem.at[1, k]),
         )
 
-    for i, (k, p) in enumerate(chunks):
-        if p == 0:
-            for copy in side(k):
-                copy.start()
-        load(i).start()
+    def load_kind(kind):
+        for copy in side(kind):
+            copy.start()
+        for i, (k, p) in enumerate(chunks):
+            if k == kind:
+                load(i).start()
+
+    load_kind(order[0])
+
+    barrier = pltpu.get_barrier_semaphore()
+
+    @pl.when(has_up)
+    def _():
+        pl.semaphore_signal(barrier, inc=1, device_id={"rows": z + 1}, device_id_type=MESH)
+
+    @pl.when(has_down)
+    def _():
+        pl.semaphore_signal(barrier, inc=1, device_id={"rows": z - 1}, device_id_type=MESH)
+
+    for step in range(1, tps):
+        pl.semaphore_signal(barrier, inc=1, device_id={"tp": lax.rem(t + step, tps)}, device_id_type=MESH)
+
+    for kind in order[1:]:
+        load_kind(kind)
 
     norm_loads = [
         pltpu.make_async_copy(source, norm_own.at[j], norm_sem.at[j])
@@ -171,10 +177,10 @@
             low_rows[k][...] = low_own[k][...].astype(jnp.float32).T.astype(jnp.bfloat16)
         load(i).wait()
         merge(i)
-        if i == 0:
+        if i == 1:
             partners = has_up.astype(jnp.int32) + has_down.astype(jnp.int32) + tps - 1
             pl.semaphore_wait(barrier, partners)
-        else:
+        if i > 0:
             send_both(functools.partial(hop, i - 1, z))
         if i == 1:
             for copy in norm_loads:
@@ -224,8 +230,10 @@
     def all_norms():
         for step in range(1, tps):
             cross(step, lax.rem(t + tps - step, tps)).wait_recv()
+        line = jnp.concatenate([norm_all[a, b] for a in range(n) for b in range(tps)], axis=1)
+        width = norm_out.shape[1]
         norm_out[...] = jnp.concatenate(
-            [norm_all[a, b] for a in range(n) for b in range(tps)], axis=1
+            [line[:, a * width : (a + 1) * width] for a in range(norm_out.shape[0])], axis=0
         ).astype(jnp.bfloat16)
 
     lax.fori_loop(1, n, distance, 0)
@@ -292,13 +300,15 @@
         else:
             shapes.append((n * rows, columns))
     share = norm_train.shape[1]
+    total = n * tps * share
+    width = 128 if total % 128 == 0 else total
     vmem, hbm = pl.BlockSpec(memory_space=pltpu.VMEM), pl.BlockSpec(memory_space=pltpu.HBM)
     dma = pltpu.SemaphoreType.DMA
     operands = (*w, *low, *high, norm_train, norm_step)
     results = pl.pallas_call(
         functools.partial(kernel, n, tps, stacked, pieces),
         out_shape=[pltpu.VMEM(s, jnp.bfloat16) for s in shapes]
-        + [pltpu.VMEM((1, n * tps * share), jnp.bfloat16)],
+        + [pltpu.VMEM((total // width, width), jnp.bfloat16)],
         in_specs=[hbm] * (3 * kinds + 2),
         out_specs=[vmem] * (kinds + 1),
         scratch_shapes=[pltpu.VMEM(x.shape, x.dtype) for x in (*w, *low, *high)]

time: 226 us -> 225 us (level)
  no operation moved by 1% of the time
where the time goes in v3:
time: 225 us
  Pallas kernels  224 us (100%)
    pallas_call x1, Pallas kernels, shards(): pl.pallas_call(functools.partial(kernel, n, tps, stacked, pieces), out_sh...  219 us
    pallas_call x1, Pallas kernels, place(): pl.pallas_call(functools.partial(put, parts), out_shape=[jax.ShapeDtypeSt...  4.91 us

profile of v3, /device:TPU:0, one launch (start us, length us, event | category | flops | bytes accessed | tf_op | source)
XLA Modules:
  0.0 224.7 jit_solution(569372083748523800)
XLA Ops:
  0.6 219.1 %merge_and_gather.1 = (bf16[2560,1024]{1,0:T(8,128)(2,1)S(1)}, bf16[2560,256]{1,0:T(8,128)(2,1)S(1)}, bf16[2560,256]{1,0:T(8,128)(2,1)S(1)}, bf16[1024,2560]{1,0:T(8,128)(2,1)S(1)}, bf16[20,128]{1,0:T(8,128)(2,1)S(1)}) custom-call(bf16[640,1024]{1,0:T(8,128)(2,1)} %refs_0_.1, bf16[640,256]{1,0:T(8,128)(2,1)} %refs_1_.1, bf16[640,256]{1,0:T(8,128)(2,1)} %refs_2_.1, ...), custom_call_target="tpu_custom_call" | custom-call | tf_op jit(solution)/shard_map/merge_and_gather/pallas_call | solution.py:308
  219.7 4.9 %place.1 = (bf16[2560,1024]{1,0:T(8,128)(2,1)}, bf16[2560,256]{1,0:T(8,128)(2,1)}, bf16[2560,256]{1,0:T(8,128)(2,1)}, bf16[1024,2560]{1,0:T(8,128)(2,1)}, bf16[20,128]{1,0:T(8,128)(2,1)}) custom-call(bf16[2560,1024]{1,0:T(8,128)(2,1)S(1)} %get-tuple-element.15.refs_0_, bf16[2560,256]{1,0:T(8,128)(2,1)S(1)} %get-tuple-element.16.refs_1_, ...), custom_call_target="tpu_custom_call" | custom-call | tf_op jit(solution)/shard_map/place/pallas_call | solution.py:274

commit v4 on v3

--- a/solution.py
+++ b/solution.py
@@ -9,7 +9,7 @@
 
 MESH = pl.DeviceIdType.MESH
 mix_rate = 0.5
-chunk_bytes = 400 * 1024
+chunk_bytes = 700 * 1024
 first_bytes = 100 * 1024
 order = (1, 0, 3, 2)
 
@@ -38,7 +38,7 @@
     w_own, low_own, high_own = refs[:kinds], refs[kinds : 2 * kinds], refs[2 * kinds : 3 * kinds]
     low_rows = refs[3 * kinds : 4 * kinds]
     refs = refs[4 * kinds :]
-    norm_own, norm_all, norm_sem, load_sem, side_sem, send_sem, recv_sem, norm_send, norm_recv, cross_send, cross_recv = refs
+    norm_own, norm_all, norm_sem, load_sem, side_sem, send_sem, recv_sem, pass_send, pass_recv, norm_send, norm_recv, cross_send, cross_recv = refs
 
     z, t = lax.axis_index("rows"), lax.axis_index("tp")
     chunks = [(k, p) for k in order for p in range(pieces[k])]
@@ -94,7 +94,7 @@
         copy.start()
 
     def region(k, p, origin):
-        start, size = rows_of(k, p)
+        start, size = (0, w[k].shape[0]) if p is None else rows_of(k, p)
         columns = w[k].shape[1]
         if stacked[k]:
             return out[k].at[origin, pl.ds(start, size)]
@@ -103,16 +103,26 @@
             return out[k].at[pl.ds(pl.multiple_of(origin * rows + start, 16), size)]
         return out[k].at[pl.ds(start, size), pl.ds(pl.multiple_of(origin * columns, 128), columns)]
 
-    def hop(i, origin, direction):
-        k, p = chunks[i]
-        place = region(k, p, origin)
+    def hop(place, send, recv, direction):
         return pltpu.make_async_remote_copy(
             src_ref=place,
             dst_ref=place,
-            send_sem=send_sem.at[direction, origin, i],
-            recv_sem=recv_sem.at[direction, origin, i],
+            send_sem=send,
+            recv_sem=recv,
             device_id={"rows": z + 1 - 2 * direction},
             device_id_type=MESH,
+        )
+
+    def chunk_hop(i, origin, direction):
+        k, p = chunks[i]
+        return hop(region(k, p, origin), send_sem.at[direction, i], recv_sem.at[direction, i], direction)
+
+    def whole_hop(k, origin, direction):
+        return hop(
+            region(k, None, origin),
+            pass_send.at[direction, origin, k],
+            pass_recv.at[direction, origin, k],
+            direction,
         )
 
     def norm_hop(origin, direction):
@@ -181,50 +191,56 @@
             partners = has_up.astype(jnp.int32) + has_down.astype(jnp.int32) + tps - 1
             pl.semaphore_wait(barrier, partners)
         if i > 0:
-            send_both(functools.partial(hop, i - 1, z))
+            send_both(functools.partial(chunk_hop, i - 1, z))
         if i == 1:
             for copy in norm_loads:
                 copy.wait()
             norm_all[z, t] = (norm_own[0] + norm_own[1]).astype(jnp.bfloat16).astype(jnp.float32)
         if i == min(2, len(chunks) - 1):
             send_both(functools.partial(norm_hop, z))
-    send_both(functools.partial(hop, len(chunks) - 1, z))
-
-    def arrival(make, d):
+    send_both(functools.partial(chunk_hop, len(chunks) - 1, z))
+
+    def arrival(arrived, onward, d):
         below, above = z - d, z + d
 
         @pl.when(below >= 0)
         def _():
-            make(below, 0).wait_recv()
+            for make in arrived:
+                make(below, 0).wait_recv()
 
             @pl.when(has_up)
             def _():
-                make(below, 0).start()
+                onward(below, 0).start()
 
         @pl.when(above < n)
         def _():
-            make(above, 1).wait_recv()
+            for make in arrived:
+                make(above, 1).wait_recv()
 
             @pl.when(has_down)
             def _():
-                make(above, 1).start()
-
-    def distance(d, _):
-        arrival(norm_hop, d)
+                onward(above, 1).start()
+
+    def distance(d, _, near=False):
+        arrival([norm_hop], norm_hop, d)
 
         @pl.when(d == n - 1)
         def _():
             for step in range(1, tps):
                 cross(step, t).start()
 
-        for i in range(len(chunks)):
-            if i == len(chunks) // 2:
+        for k in order:
+            onward = functools.partial(whole_hop, k)
+            arrived = [onward]
+            if near:
+                arrived = [functools.partial(chunk_hop, i) for i, c in enumerate(chunks) if c[0] == k]
+            if k == order[-1]:
 
                 @pl.when(d == n - 1)
                 def _():
                     all_norms()
 
-            arrival(functools.partial(hop, i), d)
+            arrival(arrived, onward, d)
         return 0
 
     def all_norms():
@@ -236,15 +252,24 @@
             [line[:, a * width : (a + 1) * width] for a in range(norm_out.shape[0])], axis=0
         ).astype(jnp.bfloat16)
 
-    lax.fori_loop(1, n, distance, 0)
+    distance(jnp.int32(1), 0, near=True)
+    lax.fori_loop(2, n, distance, 0)
+
+    for direction, flag in ((0, has_up), (1, has_down)):
+
+        @pl.when(flag)
+        def _():
+            for i in range(len(chunks)):
+                chunk_hop(i, z, direction).wait_send()
+            norm_hop(z, direction).wait_send()
 
     def drain(origin, _):
-        for direction, flag in ((0, has_up & (origin <= z)), (1, has_down & (origin >= z))):
+        for direction, flag in ((0, has_up & (origin < z)), (1, has_down & (origin > z))):
 
             @pl.when(flag)
             def _():
-                for i in range(len(chunks)):
-                    hop(i, origin, direction).wait_send()
+                for k in range(kinds):
+                    whole_hop(k, origin, direction).wait_send()
                 norm_hop(origin, direction).wait_send()
 
         return 0
@@ -270,7 +295,7 @@
 
 
 def place(arrays):
-    parts = [4 if x.shape[0] % 128 == 0 else 1 for x in arrays]
+    parts = [2 if x.shape[0] % 128 == 0 else 1 for x in arrays]
     return pl.pallas_call(
         functools.partial(put, parts),
         out_shape=[jax.ShapeDtypeStruct(x.shape, x.dtype) for x in arrays],
@@ -319,8 +344,10 @@
             dma((2,)),
             dma((count,)),
             dma((2, kinds)),
-            dma((2, n, count)),
-            dma((2, n, count)),
+            dma((2, count)),
+            dma((2, count)),
+            dma((2, n, kinds)),
+            dma((2, n, kinds)),
             dma((2, n)),
             dma((2, n)),
             dma((tps,)),

time: 225 us -> 224 us (level)
  no operation moved by 1% of the time
where the time goes in v4:
time: 224 us
  Pallas kernels  223 us (100%)
    pallas_call x1, Pallas kernels, shards(): pl.pallas_call(functools.partial(kernel, n, tps, stacked, pieces), out_sh...  218 us
    pallas_call x1, Pallas kernels, place(): pl.pallas_call(functools.partial(put, parts), out_shape=[jax.ShapeDtypeSt...  4.88 us

profile of v4, /device:TPU:0, one launch (start us, length us, event | category | flops | bytes accessed | tf_op | source)
XLA Modules:
  0.0 223.6 jit_solution(16730859774028980281)
XLA Ops:
  0.6 218.0 %merge_and_gather.1 = (bf16[2560,1024]{1,0:T(8,128)(2,1)S(1)}, bf16[2560,256]{1,0:T(8,128)(2,1)S(1)}, bf16[2560,256]{1,0:T(8,128)(2,1)S(1)}, bf16[1024,2560]{1,0:T(8,128)(2,1)S(1)}, bf16[20,128]{1,0:T(8,128)(2,1)S(1)}) custom-call(bf16[640,1024]{1,0:T(8,128)(2,1)} %refs_0_.1, bf16[640,256]{1,0:T(8,128)(2,1)} %refs_1_.1, bf16[640,256]{1,0:T(8,128)(2,1)} %refs_2_.1, ...), custom_call_target="tpu_custom_call" | custom-call | tf_op jit(solution)/shard_map/merge_and_gather/pallas_call | solution.py:333
  218.7 4.9 %place.1 = (bf16[2560,1024]{1,0:T(8,128)(2,1)}, bf16[2560,256]{1,0:T(8,128)(2,1)}, bf16[2560,256]{1,0:T(8,128)(2,1)}, bf16[1024,2560]{1,0:T(8,128)(2,1)}, bf16[20,128]{1,0:T(8,128)(2,1)}) custom-call(bf16[2560,1024]{1,0:T(8,128)(2,1)S(1)} %get-tuple-element.15.refs_0_, bf16[2560,256]{1,0:T(8,128)(2,1)S(1)} %get-tuple-element.16.refs_1_, ...), custom_call_target="tpu_custom_call" | custom-call | tf_op jit(solution)/shard_map/place/pallas_call | solution.py:299

commit v5 on v4

--- a/solution.py
+++ b/solution.py
@@ -10,7 +10,7 @@
 MESH = pl.DeviceIdType.MESH
 mix_rate = 0.5
 chunk_bytes = 700 * 1024
-first_bytes = 100 * 1024
+first_bytes = 200 * 1024
 order = (1, 0, 3, 2)
 
 
@@ -313,7 +313,8 @@
     kinds = len(w)
     by_column = [False] * (kinds - 1) + [True]
     stacked = [by_column[k] and w[k].shape[1] % 128 != 0 for k in range(kinds)]
-    pieces = [pieces_of(*w[k].shape, first_bytes if k == order[0] else chunk_bytes) for k in range(kinds)]
+    most = {order[0]: first_bytes, order[1]: chunk_bytes}
+    pieces = [pieces_of(*w[k].shape, most.get(k, w[k].size * 2)) for k in range(kinds)]
     count = sum(pieces)
     shapes = []
     for k in range(kinds):

time: 224 us -> 224 us (level)
  no operation moved by 1% of the time
where the time goes in v5:
time: 224 us; the launch traced here: 223 us
  Pallas kernels  223 us (100%)
    pallas_call x1, Pallas kernels, shards(): pl.pallas_call(functools.partial(kernel, n, tps, stacked, pieces), out_sh...  218 us
    pallas_call x1, Pallas kernels, place(): pl.pallas_call(functools.partial(put, parts), out_shape=[jax.ShapeDtypeSt...  4.88 us

profile of v5, /device:TPU:0, one launch (start us, length us, event | category | flops | bytes accessed | tf_op | source)
XLA Modules:
  0.0 223.4 jit_solution(4210453455522618952)
XLA Ops:
  0.6 217.8 %merge_and_gather.1 = (bf16[2560,1024]{1,0:T(8,128)(2,1)S(1)}, bf16[2560,256]{1,0:T(8,128)(2,1)S(1)}, bf16[2560,256]{1,0:T(8,128)(2,1)S(1)}, bf16[1024,2560]{1,0:T(8,128)(2,1)S(1)}, bf16[20,128]{1,0:T(8,128)(2,1)S(1)}) custom-call(bf16[640,1024]{1,0:T(8,128)(2,1)} %refs_0_.1, bf16[640,256]{1,0:T(8,128)(2,1)} %refs_1_.1, bf16[640,256]{1,0:T(8,128)(2,1)} %refs_2_.1, ...), custom_call_target="tpu_custom_call" | custom-call | tf_op jit(solution)/shard_map/merge_and_gather/pallas_call | solution.py:334
  218.5 4.9 %place.1 = (bf16[2560,1024]{1,0:T(8,128)(2,1)}, bf16[2560,256]{1,0:T(8,128)(2,1)}, bf16[2560,256]{1,0:T(8,128)(2,1)}, bf16[1024,2560]{1,0:T(8,128)(2,1)}, bf16[20,128]{1,0:T(8,128)(2,1)}) custom-call(bf16[2560,1024]{1,0:T(8,128)(2,1)S(1)} %get-tuple-element.15.refs_0_, bf16[2560,256]{1,0:T(8,128)(2,1)S(1)} %get-tuple-element.16.refs_1_, ...), custom_call_target="tpu_custom_call" | custom-call | tf_op jit(solution)/shard_map/place/pallas_call | solution.py:299
